TPU v7x, 256 devices: a whole 4x4x8 slice. The times are simulated.
256 devices in a mesh: dp: 32 (over x, z), mp: 8 (over y, core).
Axes of the slice: x: 4, y: 4, z: 8, core: 2. Of those that a mesh axis runs over, the one named last changes fastest.
Arguments:
- query_emb: bfloat16 [8192, 768], P('dp'), may hold values from -6 to 6
- positive_list: int32 [8192], replicated, may hold values from 0 to 32767
- centroids: float32 [32768, 768], P(('dp', 'mp')), may hold values from -0.6 to 0.6
- first_moment: float32 [32768, 768], P(('dp', 'mp')), may hold values from -3 to 3
- second_moment: float32 [32768, 768], P(('dp', 'mp')), may hold values from 0.05 to 2
Outputs:
- new_centroids: float32 [32768, 768], P(('dp', 'mp'))
- new_first: float32 [32768, 768], P(('dp', 'mp'))
- new_second: float32 [32768, 768], P(('dp', 'mp'))
- mean_loss: float32 [], replicated
All inputs are finite; a program needn't handle non-finite values.
Results may differ from a plain program's by a relative error of at most 0.00097.
Values may be sent and summed in bfloat16 or wider, within the bound.
No kernel may reach another device: no remote copies, remote signals or barrier semaphores. Data moves between devices by JAX's collectives and lax.ppermute only.
A program may use at most 64 MiB of HBM per device.

v0:
```python
import jax
import jax.numpy as jnp
from jax import lax
from jax.sharding import Mesh
from jax.sharding import PartitionSpec as P

MP = ("mp_0", "mp_1")
DP = ("dp_0", "dp_1")
DP_MP = ("dp_0", "dp_1", "mp_0", "mp_1")
beta_first = 0.9
beta_second = 0.95
learn_rate = 0.01
epsilon = 1e-08


def all_in_one(x, axis):
    leaves = jax.tree.leaves(x)
    turns = sorted(range(len(leaves)), key=lambda k: -leaves[k].size)
    width = (1, *leaves[turns[0]].shape)[-1]
    lines = [
        jnp.pad(leaves[k].reshape(-1), (0, -leaves[k].size % width)).reshape(-1, width)
        for k in turns
    ]
    both, at, found = (lax.all_gather(jnp.concatenate(lines), axis), 0, {})
    for k, line in zip(turns, lines):
        piece = both[:, at : at + len(line)].reshape(len(both), -1)
        found[k] = piece[:, : leaves[k].size].reshape(-1, *leaves[k].shape)
        at += len(line)
    numbers = iter(range(len(leaves)))
    return jax.tree.map(lambda _: found[next(numbers)], x)


def combined_by_axis(x, axes, combine):
    for axis in axes:
        pieces = all_in_one(x, axis)
        x = jax.tree.map(lambda part: part[0], pieces)
        for k in range(1, lax.axis_size(axis)):
            x = combine(x, jax.tree.map(lambda part: part[k], pieces))
    return x


def adam_update(centroids, first_moment, second_moment, gradient):
    new_first = beta_first * first_moment + (1.0 - beta_first) * gradient
    new_second = beta_second * second_moment + (1.0 - beta_second) * gradient * gradient
    new_centroids = centroids - learn_rate * new_first / (jnp.sqrt(new_second) + epsilon)
    return (new_centroids, new_first, new_second)


def combine(left_part, right_part):
    top_value = jnp.maximum(left_part[0], right_part[0])
    summed = left_part[1] * jnp.exp(left_part[0] - top_value) + right_part[1] * jnp.exp(
        right_part[0] - top_value
    )
    return (top_value, summed, left_part[2] + right_part[2])


def target_logit(logits, is_target):
    return jnp.sum(jnp.where(is_target, logits, jnp.zeros_like(logits)), axis=1)


def row_terms(logits, is_target, row_peak, row_mass, row_target):
    log_norm = row_peak + jnp.log(row_mass)
    row_loss = log_norm - row_target
    weights = (jnp.exp(logits - log_norm[:, None]) - is_target.astype(jnp.float32)).astype(
        jnp.bfloat16
    )
    return (row_loss, weights)


def shards(query_emb, positive_list, centroids, first_moment, second_moment):
    table_half = centroids.astype(jnp.bfloat16)
    own_lists = centroids.shape[0]
    count_mp = lax.axis_size(MP)
    dp_index = lax.axis_index(DP)
    mp_index = lax.axis_index(MP)
    gathered = lax.all_gather(query_emb, DP, axis=0, tiled=True)
    logits = jnp.einsum("rd,kd->rk", gathered, table_half, preferred_element_type=jnp.float32)
    shard_block = dp_index * count_mp + mp_index
    global_col = shard_block * own_lists + lax.iota(jnp.int32, own_lists)
    is_target = global_col[None, :] == positive_list[:, None]
    local_peak = jnp.max(logits, axis=1)
    local_mass = jnp.sum(jnp.exp(logits - local_peak[:, None]), axis=1)
    row_peak, row_mass, row_target = combined_by_axis(
        (local_peak, local_mass, target_logit(logits, is_target)), DP_MP, combine
    )
    row_loss, weights = row_terms(logits, is_target, row_peak, row_mass, row_target)
    mean_loss = jnp.mean(row_loss)
    gradient = jnp.einsum("rk,rd->kd", weights, gathered, preferred_element_type=jnp.float32)
    new_centroids, new_first, new_second = adam_update(
        centroids, first_moment, second_moment, gradient
    )
    return (new_centroids, new_first, new_second, mean_loss)


def solution(mesh):
    split = Mesh(mesh.devices.reshape(4, 8, 4, 2), ("dp_0", "dp_1", "mp_0", "mp_1"))
    placed = (P(DP, None), P(), P(DP_MP, None), P(DP_MP, None), P(DP_MP, None))
    return jax.shard_map(
        shards,
        mesh=split,
        in_specs=placed,
        out_specs=(P(DP_MP, None), P(DP_MP, None), P(DP_MP, None), P()),
        check_vma=False,
    )
```

profile of v0, /device:TPU:1, one launch (start us, length us, event | category | flops | bytes accessed | tf_op | source)
XLA Modules:
  0.0 219.7 jit_solution(9997302614362853183)
XLA Ops:
  7.2 0.0 all-gather.10.cloned.1.call-start
  7.2 0.7 all-gather.10.cloned.1.call-update
  7.9 0.0 copy-start.4
  7.9 124.4 %all-gather.10.cloned.1.call-done = bf16[8192,768]{1,0:T(8,128)(2,1)} async-done(((bf16[256,768]{1,0:T(8,128)(2,1)}), bf16[8192,768]{1,0:T(8,128)(2,1)}) %all-gather.10.cloned.1.call-update) | async-done | bytes 12582928 | tf_op jit(solution)/shard_map/all_gather | solution.py:76
  132.3 8.7 %fusion.73 = (f32[8192]{0:T(1024)S(1)}, f32[8192,128]{0,1:T(8,128)S(1)}) fusion(bf16[8192,768]{1,0:T(8,128)(2,1)} %all-gather.10.cloned.1.call-done, f32[128,768]{1,0:T(8,128)} %param.7), kind=kOutput, calls=%fused_computation.128 | convolution fusion | flops 1611751424 | bytes 17203200 | tf_op jit(solution)/shard_map/rd,kd->rk/dot_general | solution.py:77
  141.0 0.0 copy-start
  141.0 0.0 copy-done.4
  141.1 1.1 exponential_reduce_fusion
  142.1 0.0 copy-start.1
  142.1 0.0 copy-start.2
  142.1 0.0 copy-start.3
  142.2 0.1 maximum_bitcast_fusion
  142.3 10.2 %all-gather.4 = f32[4,3,8192]{2,1,0:T(4,128)S(1)} all-gather(f32[1,3,8192]{2,1,0:T(4,128)S(1)} %maximum_bitcast_fusion), channel_id=2, replica_groups=mesh['dp_0'=4,'dp_1'=8,'mp_0'=4,'mp_1'=2] {'dp_0'}, dimensions={0}, use_global_device_ids=true | all-gather | bytes 491520 | tf_op jit(solution)/shard_map/all_gather | solution.py:24
  152.5 0.1 fusion.43
  152.6 0.3 fusion.45
  153.0 0.1 maximum_bitcast_fusion.1
  153.1 21.0 %all-gather.5 = f32[8,3,8192]{2,1,0:T(4,128)S(1)} all-gather(f32[1,3,8192]{2,1,0:T(4,128)S(1)} %maximum_bitcast_fusion.1), channel_id=3, replica_groups=mesh['dp_0'=4,'dp_1'=8,'mp_0'=4,'mp_1'=2] {'dp_1'}, dimensions={0}, use_global_device_ids=true | all-gather | bytes 884736 | tf_op jit(solution)/shard_map/all_gather | solution.py:24
  174.0 0.2 fusion.21
  174.2 0.7 fusion.23
  175.0 0.1 maximum_bitcast_fusion.2
  175.1 10.5 %all-gather.6 = f32[4,3,8192]{2,1,0:T(4,128)S(1)} all-gather(f32[1,3,8192]{2,1,0:T(4,128)S(1)} %maximum_bitcast_fusion.2), channel_id=4, replica_groups=mesh['dp_0'=4,'dp_1'=8,'mp_0'=4,'mp_1'=2] {'mp_0'}, dimensions={0}, use_global_device_ids=true | all-gather | bytes 491520 | tf_op jit(solution)/shard_map/all_gather | solution.py:24
  185.6 0.0 copy-done
  185.6 0.1 fusion.11
  185.7 0.3 fusion.13
  186.1 0.1 maximum_bitcast_fusion.3
  186.2 14.9 %all-gather.7 = f32[2,3,8192]{2,1,0:T(4,128)S(1)} all-gather(f32[1,3,8192]{2,1,0:T(4,128)S(1)} %maximum_bitcast_fusion.3), channel_id=5, replica_groups=mesh['dp_0'=4,'dp_1'=8,'mp_0'=4,'mp_1'=2] {'mp_1'}, dimensions={0}, use_global_device_ids=true | all-gather | bytes 294912 | tf_op jit(solution)/shard_map/all_gather | solution.py:24
  201.1 0.1 fusion.72
  201.2 0.6 subtract_reduce_fusion
  202.5 0.0 copy-done.1
  202.5 0.0 copy-done.2
  202.5 0.0 copy-done.3
  202.5 9.2 %divide_subtract_fusion = (f32[128,768]{1,0:T(8,128)}, f32[128,768]{1,0:T(8,128)}, f32[128,768]{1,0:T(8,128)}) fusion(f32[128,768]{1,0:T(8,128)S(1)} %copy-done.1, f32[128,768]{1,0:T(8,128)S(1)} %copy-done.2, f32[128,768]{1,0:T(8,128)S(1)} %copy-done.3, bf16[8192,768]{1,0:T(8,128)(2,1)} %all-gather.10.cloned.1.call-done, f32[8192,128]{0,1:T(8,128)} %copy-done, ...), kind=kOutput, calls=%fused_computation.12 | convolution fusion | flops 1616936960 | bytes 19202560 | tf_op jit(solution)/shard_map/rk,rd->kd/dot_general | solution.py:88
  (1 shorter events, 0.0 us)
Async XLA Ops:
  7.2 125.2 %all-gather.10.cloned.1.call-start = ((), (), s32[]{:S(2)}) async-start(), calls=%async_computation | async-start | bytes 12976128 | tf_op jit(solution)/shard_map/all_gather | solution.py:76
  7.9 133.1 %copy-start.4 = (s32[8192]{0:T(1024)S(1)}, s32[8192]{0:T(1024)}, u32[]{:S(2)}) copy-start(s32[8192]{0:T(1024)} %param.6) | copy-start | bytes 98308
  141.0 44.6 %copy-start = (f32[8192,128]{0,1:T(8,128)}, f32[8192,128]{0,1:T(8,128)S(1)}, u32[]{:S(2)}) copy-start(f32[8192,128]{0,1:T(8,128)S(1)} %get-tuple-element.23) | copy-start | bytes 12582916
  142.1 60.4 %copy-start.1 = (f32[128,768]{1,0:T(8,128)S(1)}, f32[128,768]{1,0:T(8,128)}, u32[]{:S(2)}) copy-start(f32[128,768]{1,0:T(8,128)} %param.7) | copy-start | bytes 1179652
  142.1 60.4 %copy-start.2 = (f32[128,768]{1,0:T(8,128)S(1)}, f32[128,768]{1,0:T(8,128)}, u32[]{:S(2)}) copy-start(f32[128,768]{1,0:T(8,128)} %param.8) | copy-start | bytes 1179652
  142.1 60.4 %copy-start.3 = (f32[128,768]{1,0:T(8,128)S(1)}, f32[128,768]{1,0:T(8,128)}, u32[]{:S(2)}) copy-start(f32[128,768]{1,0:T(8,128)} %param.9) | copy-start | bytes 1179652
Sparse Core Ops, SparseCore 0:
  10.6 121.7 all-gather.9
where the time goes:
time: 220 us
  waiting for transfers between devices  125 us (57%)
  blocking collectives  56.6 us (26%)
  matrix products  17.9 us (8%)
  between operations  16 us (7%)
  other arithmetic  4.04 us (2%)
    all_gather x1, waiting for transfers between devices, shards(): gathered = lax.all_gather(query_emb, DP, axis=0, tiled=True)  124 us
    all_gather x4, blocking collectives, all_in_one(): both, at, found = (lax.all_gather(jnp.concatenate(lines), axis), 0, {})  56.6 us
    dot_general x1, matrix products, shards(): jnp.einsum('rk,rd->kd', weights, gathered, preferred_element_type=jnp.flo...  9.24 us
    dot_general x1, matrix products, shards(): jnp.einsum('rd,kd->rk', gathered, table_half, preferred_element_type=jnp....  8.7 us
  transfers between devices with their start and end apart: 1, of which 1 were waited for; matrix products, arithmetic and copies ran while one was open for 0% of the time, Pallas kernels for 0%

commit v1 on v0

--- a/solution.py
+++ b/solution.py
@@ -73,7 +73,8 @@
     count_mp = lax.axis_size(MP)
     dp_index = lax.axis_index(DP)
     mp_index = lax.axis_index(MP)
-    gathered = lax.all_gather(query_emb, DP, axis=0, tiled=True)
+    sent = jnp.stack([query_emb] * lax.axis_size(DP))
+    gathered = jnp.concatenate(lax.all_to_all(sent, DP, 0, 0), axis=0)
     logits = jnp.einsum("rd,kd->rk", gathered, table_half, preferred_element_type=jnp.float32)
     shard_block = dp_index * count_mp + mp_index
     global_col = shard_block * own_lists + lax.iota(jnp.int32, own_lists)

time: 220 us -> 397 us (1.80)
  waiting for transfers between devices: 125 us -> 280 us
  blocking collectives: 56.6 us -> 72.6 us
  between operations: 16 us -> 2.56 us
  starting transfers between devices: 0.04 us -> 12.1 us
  local copies, waits for them, and re-layouts: 0.03 us -> 6.91 us
    all_to_all x0 -> x1, waiting for transfers between devices: none -> 280 us  [shards(): gathered = jnp.concatenate(lax.all_to_all(sent, DP, 0, 0), axis=0)]
    all_gather x1 -> x0, waiting for transfers between devices: 124 us -> none  [shards(): gathered = lax.all_gather(query_emb, DP, axis=0, tiled=True)]
    all_gather x4, blocking collectives: 56.6 us -> 72.6 us  [all_in_one(): both, at, found = (lax.all_gather(jnp.concatenate(lines), axis), 0, {})]
    all_to_all x0 -> x1, starting transfers between devices: none -> 12.1 us  [shards(): gathered = jnp.concatenate(lax.all_to_all(sent, DP, 0, 0), axis=0)]
    another operation x0 -> x1, local copies, waits for them, and re-layouts: none -> 6.89 us  [shards(): sent = jnp.stack([query_emb] * lax.axis_size(DP))]
where the time goes in v1:
time: 397 us
  waiting for transfers between devices  280 us (71%)
  blocking collectives  72.6 us (18%)
  matrix products  17.9 us (5%)
  starting transfers between devices  12.1 us (3%)
  local copies, waits for them, and re-layouts  6.91 us (2%)
  other arithmetic  4.04 us (1%)
    all_to_all x1, waiting for transfers between devices, shards(): gathered = jnp.concatenate(lax.all_to_all(sent, DP, 0, 0), axis=0)  280 us
    all_gather x4, blocking collectives, all_in_one(): both, at, found = (lax.all_gather(jnp.concatenate(lines), axis), 0, {})  72.6 us
    all_to_all x1, starting transfers between devices, shards(): gathered = jnp.concatenate(lax.all_to_all(sent, DP, 0, 0), axis=0)  12.1 us
    dot_general x1, matrix products, shards(): jnp.einsum('rk,rd->kd', weights, gathered, preferred_element_type=jnp.flo...  9.23 us
    dot_general x1, matrix products, shards(): jnp.einsum('rd,kd->rk', gathered, table_half, preferred_element_type=jnp....  8.72 us
  transfers between devices with their start and end apart: 1, of which 1 were waited for; matrix products, arithmetic and copies ran while one was open for 0% of the time, Pallas kernels for 0%

profile of v1, /device:TPU:1, one launch (start us, length us, event | category | flops | bytes accessed | tf_op | source)
XLA Modules:
  0.0 396.7 jit_solution(9850300474844215375)
XLA Ops:
  0.6 6.9 %stack.2 = bf16[32,256,768]{2,1,0:T(8,128)(2,1)} broadcast(bf16[256,768]{1,0:T(8,128)(2,1)} %param.5), dimensions={1,2} | broadcast | bytes 12976128 | tf_op jit(solution)/shard_map/stack | solution.py:76
  7.5 0.0 copy-start.1
  7.5 12.1 %all-to-all-start = ((bf16[32,256,768]{2,1,0:T(8,128)(2,1)}), bf16[32,256,768]{2,1,0:T(8,128)(2,1)}, u32[]{:S(2)}, u32[]{:S(2)}) async-start(bf16[32,256,768]{2,1,0:T(8,128)(2,1)} %stack.2), calls=%async_computation | async-start | bytes 25165824 | tf_op jit(solution)/shard_map/all_to_all | solution.py:77
  19.6 280.5 %all-to-all-done = bf16[32,256,768]{2,1,0:T(8,128)(2,1)} async-done(((bf16[32,256,768]{2,1,0:T(8,128)(2,1)}), bf16[32,256,768]{2,1,0:T(8,128)(2,1)}, u32[]{:S(2)}, u32[]{:S(2)}) %all-to-all-start) | async-done | bytes 12582944 | tf_op jit(solution)/shard_map/all_to_all | solution.py:77
  300.1 0.0 copy-done.1
  300.1 0.0 copy-start.4
  300.1 8.7 %fusion.73 = (f32[8192]{0:T(1024)S(1)}, f32[8192,128]{0,1:T(8,128)S(1)}) fusion(bf16[8192,768]{1,0:T(8,128)(2,1)} %bitcast, f32[128,768]{1,0:T(8,128)S(1)} %copy-done.1), kind=kOutput, calls=%fused_computation.128 | convolution fusion | flops 1611751424 | bytes 17203200 | tf_op jit(solution)/shard_map/rd,kd->rk/dot_general | solution.py:78
  308.9 0.0 copy-start
  308.9 0.0 copy-done.4
  308.9 1.1 exponential_reduce_fusion
  309.9 0.0 copy-start.2
  310.0 0.0 copy-start.3
  310.0 0.1 maximum_bitcast_fusion
  310.1 22.0 %all-gather.4 = f32[4,3,8192]{2,1,0:T(4,128)S(1)} all-gather(f32[1,3,8192]{2,1,0:T(4,128)S(1)} %maximum_bitcast_fusion), channel_id=2, replica_groups=mesh['dp_0'=4,'dp_1'=8,'mp_0'=4,'mp_1'=2] {'dp_0'}, dimensions={0}, use_global_device_ids=true | all-gather | bytes 491520 | tf_op jit(solution)/shard_map/all_gather | solution.py:24
  332.1 0.1 fusion.43
  332.2 0.3 fusion.45
  332.5 0.1 maximum_bitcast_fusion.1
  332.6 28.6 %all-gather.5 = f32[8,3,8192]{2,1,0:T(4,128)S(1)} all-gather(f32[1,3,8192]{2,1,0:T(4,128)S(1)} %maximum_bitcast_fusion.1), channel_id=3, replica_groups=mesh['dp_0'=4,'dp_1'=8,'mp_0'=4,'mp_1'=2] {'dp_1'}, dimensions={0}, use_global_device_ids=true | all-gather | bytes 884736 | tf_op jit(solution)/shard_map/all_gather | solution.py:24
  361.2 0.2 fusion.21
  361.4 0.7 fusion.23
  362.2 0.1 maximum_bitcast_fusion.2
  362.3 10.7 %all-gather.6 = f32[4,3,8192]{2,1,0:T(4,128)S(1)} all-gather(f32[1,3,8192]{2,1,0:T(4,128)S(1)} %maximum_bitcast_fusion.2), channel_id=4, replica_groups=mesh['dp_0'=4,'dp_1'=8,'mp_0'=4,'mp_1'=2] {'mp_0'}, dimensions={0}, use_global_device_ids=true | all-gather | bytes 491520 | tf_op jit(solution)/shard_map/all_gather | solution.py:24
  373.0 0.0 copy-done
  373.0 0.1 fusion.11
  373.1 0.3 fusion.13
  373.4 0.1 maximum_bitcast_fusion.3
  373.5 11.3 %all-gather.7 = f32[2,3,8192]{2,1,0:T(4,128)S(1)} all-gather(f32[1,3,8192]{2,1,0:T(4,128)S(1)} %maximum_bitcast_fusion.3), channel_id=5, replica_groups=mesh['dp_0'=4,'dp_1'=8,'mp_0'=4,'mp_1'=2] {'mp_1'}, dimensions={0}, use_global_device_ids=true | all-gather | bytes 294912 | tf_op jit(solution)/shard_map/all_gather | solution.py:24
  384.9 0.1 fusion.72
  385.0 0.6 subtract_reduce_fusion
  386.3 0.0 copy-done.2
  386.3 0.0 copy-done.3
  386.3 9.2 %divide_subtract_fusion = (f32[128,768]{1,0:T(8,128)}, f32[128,768]{1,0:T(8,128)}, f32[128,768]{1,0:T(8,128)}) fusion(f32[128,768]{1,0:T(8,128)S(1)} %copy-done.1, f32[128,768]{1,0:T(8,128)S(1)} %copy-done.2, f32[128,768]{1,0:T(8,128)S(1)} %copy-done.3, bf16[8192,768]{1,0:T(8,128)(2,1)} %bitcast, f32[8192,128]{0,1:T(8,128)} %copy-done, ...), kind=kOutput, calls=%fused_computation.12 | convolution fusion | flops 1616936960 | bytes 19202560 | tf_op jit(solution)/shard_map/rk,rd->kd/dot_general | solution.py:89
  (1 shorter events, 0.0 us)
Async XLA Ops:
  7.5 292.6 %copy-start.1 = (f32[128,768]{1,0:T(8,128)S(1)}, f32[128,768]{1,0:T(8,128)}, u32[]{:S(2)}) copy-start(f32[128,768]{1,0:T(8,128)} %param.7) | copy-start | bytes 1179652
  7.5 292.6 %all-to-all-start = ((bf16[32,256,768]{2,1,0:T(8,128)(2,1)}), bf16[32,256,768]{2,1,0:T(8,128)(2,1)}, u32[]{:S(2)}, u32[]{:S(2)}) async-start(bf16[32,256,768]{2,1,0:T(8,128)(2,1)} %stack.2), calls=%async_computation | async-start | bytes 25165824 | tf_op jit(solution)/shard_map/all_to_all | solution.py:77
  300.1 8.7 %copy-start.4 = (s32[8192]{0:T(1024)S(1)}, s32[8192]{0:T(1024)}, u32[]{:S(2)}) copy-start(s32[8192]{0:T(1024)} %param.6) | copy-start | bytes 98308
  308.9 64.1 %copy-start = (f32[8192,128]{0,1:T(8,128)}, f32[8192,128]{0,1:T(8,128)S(1)}, u32[]{:S(2)}) copy-start(f32[8192,128]{0,1:T(8,128)S(1)} %get-tuple-element.23) | copy-start | bytes 12582916
  309.9 76.3 %copy-start.2 = (f32[128,768]{1,0:T(8,128)S(1)}, f32[128,768]{1,0:T(8,128)}, u32[]{:S(2)}) copy-start(f32[128,768]{1,0:T(8,128)} %param.8) | copy-start | bytes 1179652
  310.0 76.3 %copy-start.3 = (f32[128,768]{1,0:T(8,128)S(1)}, f32[128,768]{1,0:T(8,128)}, u32[]{:S(2)}) copy-start(f32[128,768]{1,0:T(8,128)} %param.9) | copy-start | bytes 1179652
